TPU v7x, 512 devices: a 4x2x32 block of a 4x8x32 slice. The times are simulated.
512 devices in a mesh: groups: 2 (over y), seq: 32 (over z), head: 4 (over x), sub: 2 (over core).
Axes of the slice: x: 4, y: 2, z: 32, core: 2. Of those that a mesh axis runs over, the one named last changes fastest.
The devices are a block of a 4x8x32 slice.
Arguments:
- hidden: bfloat16 [8192, 7168], P(('groups', 'seq')), parts along dimension 0, may hold values from -240 to 240
- segment_ids: int32 [8192], P('groups'), parts along dimension 0, may hold values from 0 to 2, never falling along the last dimension, each value on 1 to 2048 neighbouring positions
- attn_gain: float32 [7168], replicated, may hold values from 0.1 to 1.9
- down_weight: bfloat16 [7168, 2112], P('seq', ('head', 'sub')), may hold values from -0.0625 to 0.0625
- q_gain: float32 [1536], replicated, may hold values from 0.1 to 1.9
- kv_gain: float32 [512], replicated, may hold values from 0.1 to 1.9
- q_up: bfloat16 [1536, 12288], P('seq', ('head', 'sub')), may hold values from -0.15625 to 0.15625
- key_up: bfloat16 [8192, 512], P(('head', 'sub'), 'seq'), may hold values from -8 to 8
- value_up: bfloat16 [512, 8192], P('seq', ('head', 'sub')), may hold values from -1 to 1
Outputs:
- attended: bfloat16 [8192, 8192], P(('groups', 'seq'), ('head', 'sub')), parts along dimension 0
There are 2 independent parts, one for each index of `groups`. A program takes and returns all parts, laid end to end along the dimension named above; an argument that names none is the same for every part. Nothing has to cross between parts.
Inputs may be any that keep to these rules, and one draw needn't show every extreme that they name: `segment_ids`: document numbers never fall along the pack.
All inputs are finite; a program needn't handle non-finite values.
Results may differ from a plain program's by a relative error of at most 0.014.
The roundings to bfloat16 on the way count: a program that leaves them out, or rounds other values in their place, can miss the bound.
Values may be sent and summed in bfloat16 or wider, within the bound.
A program may use at most 64 MiB of HBM per device.

v0:
```python
import functools
import math
import jax
import jax.numpy as jnp
from jax import lax
from jax.sharding import PartitionSpec as P

QL = 1536
KVL = 512
ROPE = 64
NOPE = 128
VDIM = 128
EPSILON = 1e-06
ROPE_BASE = 10000.0
LOWEST_SCORE = -1e30


def laid_out(pieces, dim):
    shape = list(pieces.shape[1:])
    shape[dim] *= pieces.shape[0]
    return jnp.moveaxis(pieces, 0, dim).reshape(shape)


def from_everyone(value, axis):
    copies = jnp.broadcast_to(value, (lax.axis_size(axis), *value.shape))
    return lax.all_to_all(copies, axis, split_axis=0, concat_axis=0, tiled=True)


def gathered_copies(value, axis, dim):
    return laid_out(from_everyone(value, axis), dim)


def rotate(values, positions):
    half_width = values.shape[-1] // 2
    frequency = ROPE_BASE ** (-jnp.arange(half_width, dtype=jnp.float32) / half_width)
    angles = positions.astype(jnp.float32)[:, None] * frequency[None, :]
    target_shape = (angles.shape[0],) + (1,) * (values.ndim - 2) + (half_width,)
    cosine = jnp.cos(angles).reshape(target_shape)
    sine_part = jnp.sin(angles).reshape(target_shape)
    leading = values[..., :half_width]
    second = values[..., half_width:]
    return jnp.concatenate(
        [leading * cosine - second * sine_part, leading * sine_part + second * cosine], axis=-1
    )


def rms_scale(values):
    return lax.rsqrt(jnp.mean(values * values, axis=-1, keepdims=True) + EPSILON)


def make_keys(columns, positions, kv_gain):
    latent_raw = columns[:, :KVL].astype(jnp.float32)
    latent = (latent_raw * rms_scale(latent_raw) * kv_gain[None, :]).astype(jnp.bfloat16)
    key_rope = rotate(columns[:, KVL:].astype(jnp.float32), positions).astype(jnp.bfloat16)
    return jnp.concatenate([latent, key_rope], axis=1)


def unchanged(carry_state):
    return carry_state


def local(hidden, segment_ids, attn_gain, down_weight, q_gain, kv_gain, q_up, key_up, value_up):
    row_count = hidden.shape[0]
    half_rows = row_count // 2
    cycle_index = lax.axis_index("seq")
    positions = cycle_index * row_count + jnp.arange(row_count, dtype=jnp.int32)
    own_segments = jnp.take(segment_ids, positions)
    widened = hidden.astype(jnp.float32)
    inverse = rms_scale(widened)
    scaled = (widened * attn_gain[None, :]).astype(jnp.bfloat16)
    chosen = scaled
    down_part = jnp.dot(
        chosen,
        lax.all_gather(down_weight, "seq", axis=0, tiled=True),
        preferred_element_type=jnp.float32,
    )
    down_part = (down_part * inverse).astype(jnp.bfloat16)
    projected = lax.all_gather(down_part, ("head", "sub"), axis=1, tiled=True)
    query_low = projected[:, :QL].astype(jnp.float32)
    query_latent = (query_low * rms_scale(query_low) * q_gain[None, :]).astype(jnp.bfloat16)
    head_count = q_up.shape[1] // (NOPE + ROPE)
    chosen = query_latent
    query_full = jnp.dot(
        chosen, lax.all_gather(q_up, "seq", axis=0, tiled=True), preferred_element_type=jnp.float32
    )
    query_full = query_full.astype(jnp.bfloat16).reshape(row_count, head_count, NOPE + ROPE)
    query_rope = rotate(query_full[:, :, NOPE:].astype(jnp.float32), positions).astype(jnp.bfloat16)
    query_nope = query_full[:, :, :NOPE]
    shard_piece = gathered_copies(key_up, "seq", 1)
    blocks = shard_piece.reshape(head_count, NOPE, shard_piece.shape[1])
    absorbed = jnp.einsum(
        "thc,hcn->thn", query_nope, blocks, preferred_element_type=jnp.float32
    ).astype(jnp.bfloat16)
    queries = jnp.concatenate([absorbed, query_rope], axis=2)
    score_scale = (NOPE + ROPE) ** (-0.5)
    halves = (queries[:half_rows], queries[half_rows:])
    half_pos = (positions[:half_rows], positions[half_rows:])
    half_seg = (own_segments[:half_rows], own_segments[half_rows:])

    def attend(carry_state, key_block, key_pos, key_seg, half_index):
        running_max, running_sum, accumulator = carry_state
        scores = (
            jnp.einsum(
                "thc,nc->htn", halves[half_index], key_block, preferred_element_type=jnp.float32
            )
            * score_scale
        )
        allowed = (key_pos[None, :] <= half_pos[half_index][:, None]) & (
            key_seg[None, :] == half_seg[half_index][:, None]
        )
        scores = jnp.where(allowed[None], scores, -jnp.inf)
        new_max = jnp.maximum(running_max, jnp.max(scores, axis=2))
        shrink = jnp.exp(running_max - new_max)
        weights = jnp.exp(scores - new_max[:, :, None])
        running_sum = running_sum * shrink + jnp.sum(weights, axis=2)
        accumulator = accumulator * shrink[:, :, None] + jnp.einsum(
            "htn,nc->htc",
            weights.astype(jnp.bfloat16),
            key_block[:, :KVL],
            preferred_element_type=jnp.float32,
        )
        return (new_max, running_sum, accumulator)

    start_state = tuple(
        (
            (
                jnp.full((head_count, half_rows), LOWEST_SCORE, jnp.float32),
                jnp.zeros((head_count, half_rows), jnp.float32),
                jnp.zeros((head_count, half_rows, KVL), jnp.float32),
            )
            for half_index in range(2)
        )
    )
    share_count = lax.axis_size(("head", "sub"))
    share_rows = row_count // share_count
    share_first = lax.axis_index(("head", "sub")) * share_rows
    own_columns = lax.dynamic_slice_in_dim(projected[:, QL:], share_first, share_rows, 0)
    own_positions = lax.dynamic_slice_in_dim(positions, share_first, share_rows, 0)
    own_keys = make_keys(own_columns, own_positions, kv_gain)
    shard_piece = gathered_copies(own_keys, "seq", 0)
    shard_total = shard_piece.shape[0] // share_rows
    stacked = shard_piece.reshape(shard_total, share_rows, shard_piece.shape[1])
    assembled = gathered_copies(stacked, ("head", "sub"), 1)
    assembled = assembled.reshape(shard_total * row_count, shard_piece.shape[1])
    piece_rows = assembled.shape[0]
    block_rows = math.gcd(piece_rows, row_count)
    blocks = assembled.reshape(piece_rows // block_rows, block_rows, assembled.shape[1])
    firsts = block_rows * jnp.arange(piece_rows // block_rows, dtype=jnp.int32)

    def visit_block(block_state, scan_item):
        key_block, block_start = scan_item
        key_pos = block_start + jnp.arange(block_rows, dtype=jnp.int32)
        key_seg = jnp.take(segment_ids, key_pos)
        updated = []
        for half_index in range(2):
            is_live = jnp.min(key_pos) <= jnp.max(half_pos[half_index])
            refresh = functools.partial(
                attend, key_block=key_block, key_pos=key_pos, key_seg=key_seg, half_index=half_index
            )
            updated.append(lax.cond(is_live, refresh, unchanged, block_state[half_index]))
        return (tuple(updated), None)

    final_state, unused = lax.scan(visit_block, start_state, (blocks, firsts))
    attended = jnp.concatenate(
        [
            (accumulator / running_sum[:, :, None]).astype(jnp.bfloat16)
            for running_max, running_sum, accumulator in final_state
        ],
        axis=1,
    )
    shard_piece = gathered_copies(value_up, "seq", 0)
    chosen = attended
    blocks = shard_piece.reshape(shard_piece.shape[0], head_count, VDIM)
    result = jnp.einsum("htn,nhv->thv", chosen, blocks, preferred_element_type=jnp.float32)
    result = result.reshape(row_count, head_count * VDIM).astype(jnp.bfloat16)
    return result


def solution(mesh):
    placed = (
        P(("groups", "seq"), None),
        P("groups"),
        P(),
        P("seq", ("head", "sub")),
        P(),
        P(),
        P("seq", ("head", "sub")),
        P(("head", "sub"), "seq"),
        P("seq", ("head", "sub")),
    )
    return jax.shard_map(
        local,
        mesh=mesh,
        in_specs=placed,
        out_specs=P(("groups", "seq"), ("head", "sub")),
        check_vma=False,
    )
```

profile of v0, /device:TPU:1952, one launch (start us, length us, event | category | flops | bytes accessed | tf_op | source)
XLA Modules:
  0.0 853.1 jit_solution(4573938176594299014)
XLA Ops:
  8.4 6.5 all-to-all-start.2
  15.7 113.6 %all-to-all-done.2 = bf16[32,1024,16]{1,2,0:T(8,128)(2,1)S(1)} async-done(((bf16[32,1024,16]{1,2,0:T(8,128)(2,1)}), bf16[32,1024,16]{1,2,0:T(8,128)(2,1)S(1)}, u32[]{:S(2)}, u32[]{:S(2)}) %all-to-all-start.2) | async-done | bytes 1048608 | tf_op jit(solution)/shard_map/all_to_all | solution.py:26
  130.4 6.3 all-to-all-start.3
  139.6 142.9 %all-gather.6.cloned.1.call-done = bf16[32,224,264]{1,2,0:T(8,128)(2,1)} async-done(((bf16[1,224,264]{1,2,0:T(8,128)(2,1)}), bf16[32,224,264]{1,2,0:T(8,128)(2,1)}) %all-gather.6.cloned.1.call-update) | async-done | bytes 3784720 | tf_op jit(solution)/shard_map/all_gather | solution.py:74
  282.5 5.3 copy.70
  287.8 9.1 %reshape.234 = bf16[7168,264]{0,1:T(8,128)(2,1)} reshape(bf16[32,224,264]{1,0,2:T(8,128)(2,1)} %copy.70) | data formatting | bytes 7569408
  296.9 3.8 fusion.28
  300.7 13.6 %all_gather.10 = bf16[128,2112]{0,1:T(8,128)(2,1)S(1)} all-gather(bf16[128,264]{0,1:T(8,128)(2,1)S(1)} %fusion.28), channel_id=1, replica_groups=mesh['groups'=2,'seq'=32,'head'=4,'sub'=2] {'head','sub'}, dimensions={1}, use_global_device_ids=true | all-gather | bytes 608256 | tf_op jit(solution)/shard_map/all_gather | solution.py:78
  315.2 94.7 %all_to_all.20 = bf16[32,16,576]{2,1,0:T(8,128)(2,1)S(1)} all-to-all(bf16[32,16,576]{2,1,0:T(8,128)(2,1)S(1)} %broadcast_in_dim.41), channel_id=1, replica_groups=mesh['groups'=2,'seq'=32,'head'=4,'sub'=2] {'seq'}, dimensions={0} | all-to-all | bytes 1179648 | tf_op jit(solution)/shard_map/all_to_all | solution.py:26
  410.0 2.7 broadcast_in_dim.42
  412.7 5.2 all-to-all-start.1
  422.0 44.1 %all-gather.4.cloned.1.call-done = bf16[1536,1536]{1,0:T(8,128)(2,1)} async-done(((bf16[48,1536]{1,0:T(8,128)(2,1)}), bf16[1536,1536]{1,0:T(8,128)(2,1)}) %all-gather.4.cloned.1.call-update) | async-done | bytes 4718608 | tf_op jit(solution)/shard_map/all_gather | solution.py:84
  466.1 3.4 convolution_convert_fusion
  472.0 6.5 all-to-all-done.1
  478.5 5.6 copy.72
  484.4 359.2 %while.21 = (s32[]{:T(128)}, f32[8,64]{1,0:T(8,128)S(1)}, f32[8,64]{1,0:T(8,128)S(1)}, f32[8,64,512]{2,1,0:T(8,128)S(1)}, f32[8,64]{1,0:T(8,128)S(1)}, /*index=5...) while((s32[]{:T(128)}, f32[8,64]{1,0:T(8,128)S(1)}, ...), condition=%wide.region_15.17_spmd, body=%wide.region_5.16_spmd.sunk | while | flops 287232768 | bytes 7917033 | solution.py:163
  493.3 2.4 conditional.4
  504.6 2.4 conditional.4
  516.0 2.4 conditional.4
  527.3 2.4 conditional.4
  538.6 2.4 conditional.4
  550.0 2.4 conditional.4
  561.3 2.4 conditional.4
  572.7 2.4 conditional.4
  606.7 2.4 conditional.4
  618.0 2.4 conditional.4
  629.4 2.4 conditional.4
  720.1 2.4 conditional.4
  731.5 2.4 conditional.4
  742.8 2.4 conditional.4
  822.2 2.4 conditional.4
  833.6 2.4 conditional.4
  (774 shorter events, 368.8 us)
Async XLA Ops:
  6.5 122.7 %copy-start.3 = (bf16[16,1024]{1,0:T(8,128)(2,1)S(1)}, bf16[16,1024]{1,0:T(8,128)(2,1)}, u32[]{:S(2)}) copy-start(bf16[16,1024]{1,0:T(8,128)(2,1)} %param.25) | copy-start | bytes 98308
  8.4 120.8 %all-to-all-start.2 = ((bf16[32,1024,16]{1,2,0:T(8,128)(2,1)}), bf16[32,1024,16]{1,2,0:T(8,128)(2,1)S(1)}, u32[]{:S(2)}, u32[]{:S(2)}) async-start(bf16[32,1024,16]{1,2,0:T(8,128)(2,1)} %broadcast_in_dim.43), calls=%async_computation.2 | async-start | bytes 2097152 | tf_op jit(solution)/shard_map/all_to_all | solution.py:26
  14.9 267.6 %all-gather.6.cloned.1.call-start = ((), (), s32[]{:S(2)}) async-start(), calls=%async_computation.5 | async-start | bytes 4460544 | tf_op jit(solution)/shard_map/all_gather | solution.py:74
  130.4 184.7 %all-to-all-start.3 = ((bf16[32,16,1024]{2,1,0:T(8,128)(2,1)}), bf16[32,16,1024]{2,1,0:T(8,128)(2,1)S(1)}, u32[]{:S(2)}, u32[]{:S(2)}) async-start(bf16[32,16,1024]{2,1,0:T(8,128)(2,1)} %broadcast_in_dim.44), calls=%async_computation.3 | async-start | bytes 2097152 | tf_op jit(solution)/shard_map/all_to_all | solution.py:26
  136.7 329.4 %all-gather.4.cloned.1.call-start = ((), (), s32[]{:S(2)}) async-start(), calls=%async_computation.4 | async-start | bytes 4866048 | tf_op jit(solution)/shard_map/all_gather | solution.py:84
  287.8 9.1 %copy-start.6 = (f32[7168]{0:T(1024)S(1)}, f32[7168]{0:T(1024)}, u32[]{:S(2)}) copy-start(f32[7168]{0:T(1024)} %param.19) | copy-start | bytes 86020
  296.9 18.1 %copy-start.5 = (f32[512]{0:T(512)S(1)}, f32[512]{0:T(512)}, u32[]{:S(2)}) copy-start(f32[512]{0:T(512)} %param.22) | copy-start | bytes 6148
  314.4 105.9 %copy-start.1 = (bf16[128,2112]{0,1:T(8,128)(2,1)}, bf16[128,2112]{0,1:T(8,128)(2,1)S(1)}, u32[]{:S(2)}) copy-start(bf16[128,2112]{0,1:T(8,128)(2,1)S(1)} %all_gather.10) | copy-start | bytes 1622020
  412.7 5.2 copy-start
  412.7 65.8 %all-to-all-start.1 = ((bf16[8,32,16,576]{3,2,1,0:T(8,128)(2,1)}), bf16[8,32,16,576]{3,2,1,0:T(8,128)(2,1)}, u32[]{:S(2)}, u32[]{:S(2)}) async-start(bf16[8,32,16,576]{3,2,1,0:T(8,128)(2,1)} %broadcast_in_dim.42), calls=%async_computation.1 | async-start | bytes 10485760 | tf_op jit(solution)/shard_map/all_to_all | solution.py:26
  417.9 48.2 %copy-start.4 = (f32[1536]{0:T(1024)S(1)}, f32[1536]{0:T(1024)}, u32[]{:S(2)}) copy-start(f32[1536]{0:T(1024)} %param.21) | copy-start | bytes 18436
  843.6 1.2 copy-start.2
Sparse Core Ops, SparseCore 0:
  17.8 264.6 all-gather.5
  284.6 181.5 all-gather.3
where the time goes:
time: 859 us; the launch traced here: 853 us
  waiting for transfers between devices  309 us (36%)
  local copies, waits for them, and re-layouts  118 us (14%)
  blocking collectives  108 us (13%)
  other arithmetic  104 us (12%)
  matrix products  97.9 us (11%)
  loops' own time  85.1 us (10%)
  starting transfers between devices  18 us (2%)
  between operations  13.8 us (2%)
    all_gather x1, waiting for transfers between devices, local(): lax.all_gather(down_weight, 'seq', axis=0, tiled=True)  143 us
    all_to_all x3, waiting for transfers between devices, from_everyone(): return lax.all_to_all(copies, axis, split_axis=0, concat_axis=0, tiled=True)  120 us
    all_to_all x1, blocking collectives, from_everyone(): return lax.all_to_all(copies, axis, split_axis=0, concat_axis=0, tiled=True)  94.7 us
    another operation x1, loops' own time, local(): final_state, unused = lax.scan(visit_block, start_state, (blocks, firsts))  81.2 us
    dot_general x62, matrix products, attend(): jnp.einsum('thc,nc->htn', halves[half_index], key_block, preferred_elemen...  59.4 us
    all_gather x1, waiting for transfers between devices, local(): lax.all_gather(q_up, 'seq', axis=0, tiled=True)  44.1 us
    reduce_min x32, other arithmetic, visit_block(): is_live = jnp.min(key_pos) <= jnp.max(half_pos[half_index])  39.4 us
    gather x32, local copies, waits for them, and re-layouts, visit_block(): key_seg = jnp.take(segment_ids, key_pos)  36.7 us
  transfers between devices with their start and end apart: 5, of which 4 were waited for; matrix products, arithmetic and copies ran while one was open for 4% of the time, Pallas kernels for 0%

commit v1 on v0

--- a/solution.py
+++ b/solution.py
@@ -13,6 +13,11 @@
 EPSILON = 1e-06
 ROPE_BASE = 10000.0
 LOWEST_SCORE = -1e30
+
+
+def swapped_in(value, mesh_axis, along):
+    sent = jnp.stack([value] * lax.axis_size(mesh_axis))
+    return jnp.concatenate(lax.all_to_all(sent, mesh_axis, 0, 0), axis=along)
 
 
 def laid_out(pieces, dim):
@@ -80,9 +85,7 @@
     query_latent = (query_low * rms_scale(query_low) * q_gain[None, :]).astype(jnp.bfloat16)
     head_count = q_up.shape[1] // (NOPE + ROPE)
     chosen = query_latent
-    query_full = jnp.dot(
-        chosen, lax.all_gather(q_up, "seq", axis=0, tiled=True), preferred_element_type=jnp.float32
-    )
+    query_full = jnp.dot(chosen, swapped_in(q_up, "seq", 0), preferred_element_type=jnp.float32)
     query_full = query_full.astype(jnp.bfloat16).reshape(row_count, head_count, NOPE + ROPE)
     query_rope = rotate(query_full[:, :, NOPE:].astype(jnp.float32), positions).astype(jnp.bfloat16)
     query_nope = query_full[:, :, :NOPE]

time: 859 us -> 1290 us (1.50)
  waiting for transfers between devices: 309 us -> 669 us
  blocking collectives: 108 us -> 164 us
    all_to_all x0 -> x1, waiting for transfers between devices: none -> 411 us  [swapped_in(): return jnp.concatenate(lax.all_to_all(sent, mesh_axis, 0, 0), axis=along)]
    all_to_all x1 -> x2, blocking collectives: 94.7 us -> 151 us  [from_everyone(): return lax.all_to_all(copies, axis, split_axis=0, concat_axis=0, tiled=True)]
    all_gather x1 -> x0, waiting for transfers between devices: 44.1 us -> none  [local(): lax.all_gather(q_up, 'seq', axis=0, tiled=True)]
    all_to_all x3 -> x2, waiting for transfers between devices: 120 us -> 114 us  [from_everyone(): return lax.all_to_all(copies, axis, split_axis=0, concat_axis=0, tiled=True)]
  transfers between devices with their start and end apart: 5 -> 4, of which waited for: 4 -> 3; matrix products, arithmetic and copies ran while one was open for 4% -> 2% of each run, Pallas kernels for 0% -> 0%
where the time goes in v1:
time: 1290 us
  waiting for transfers between devices  669 us (52%)
  blocking collectives  164 us (13%)
  local copies, waits for them, and re-layouts  121 us (9%)
  other arithmetic  109 us (8%)
  matrix products  97.7 us (8%)
  loops' own time  87.1 us (7%)
  starting transfers between devices  23.3 us (2%)
  between operations  13.8 us (1%)
    all_to_all x1, waiting for transfers between devices, swapped_in(): return jnp.concatenate(lax.all_to_all(sent, mesh_axis, 0, 0), axis=along)  411 us
    all_to_all x2, blocking collectives, from_everyone(): return lax.all_to_all(copies, axis, split_axis=0, concat_axis=0, tiled=True)  151 us
    all_gather x1, waiting for transfers between devices, local(): lax.all_gather(down_weight, 'seq', axis=0, tiled=True)  144 us
    all_to_all x2, waiting for transfers between devices, from_everyone(): return lax.all_to_all(copies, axis, split_axis=0, concat_axis=0, tiled=True)  114 us
    another operation x1, loops' own time, local(): final_state, unused = lax.scan(visit_block, start_state, (blocks, firsts))  83.2 us
    dot_general x62, matrix products, attend(): jnp.einsum('thc,nc->htn', halves[half_index], key_block, preferred_elemen...  59.3 us
    select_n x64, other arithmetic, visit_block(): key_seg = jnp.take(segment_ids, key_pos)  40.8 us
    reduce_min x32, other arithmetic, visit_block(): is_live = jnp.min(key_pos) <= jnp.max(half_pos[half_index])  40.6 us
  transfers between devices with their start and end apart: 4, of which 3 were waited for; matrix products, arithmetic and copies ran while one was open for 2% of the time, Pallas kernels for 0%

profile of v1, /device:TPU:1952, one launch (start us, length us, event | category | flops | bytes accessed | tf_op | source)
XLA Modules:
  0.0 1285.2 jit_solution(8249262806981224368)
XLA Ops:
  8.4 6.5 all-to-all-start.3
  15.7 113.6 %all-to-all-done.3 = bf16[32,1024,16]{1,2,0:T(8,128)(2,1)S(1)} async-done(((bf16[32,1024,16]{1,2,0:T(8,128)(2,1)}), bf16[32,1024,16]{1,2,0:T(8,128)(2,1)S(1)}, u32[]{:S(2)}, u32[]{:S(2)}) %all-to-all-start.3) | async-done | bytes 1048608 | tf_op jit(solution)/shard_map/all_to_all | solution.py:31
  130.4 6.3 all-to-all-start.4
  138.8 143.6 %all-gather.3.cloned.1.call-done = bf16[32,224,264]{1,2,0:T(8,128)(2,1)} async-done(((bf16[1,224,264]{1,2,0:T(8,128)(2,1)}), bf16[32,224,264]{1,2,0:T(8,128)(2,1)}) %all-gather.3.cloned.1.call-update) | async-done | bytes 3784720 | tf_op jit(solution)/shard_map/all_gather | solution.py:79
  282.4 5.3 copy.70
  287.7 9.1 reshape.240
  296.8 3.8 fusion.28
  300.7 13.6 %all_gather.7 = bf16[128,2112]{0,1:T(8,128)(2,1)S(1)} all-gather(bf16[128,264]{0,1:T(8,128)(2,1)S(1)} %fusion.28), channel_id=1, replica_groups=mesh['groups'=2,'seq'=32,'head'=4,'sub'=2] {'head','sub'}, dimensions={1}, use_global_device_ids=true | all-gather | bytes 608256 | tf_op jit(solution)/shard_map/all_gather | solution.py:83
  315.2 86.2 %all_to_all.25 = bf16[32,16,576]{2,1,0:T(8,128)(2,1)S(1)} all-to-all(bf16[32,16,576]{2,1,0:T(8,128)(2,1)S(1)} %broadcast_in_dim.41), channel_id=1, replica_groups=mesh['groups'=2,'seq'=32,'head'=4,'sub'=2] {'seq'}, dimensions={0} | all-to-all | bytes 1179648 | tf_op jit(solution)/shard_map/all_to_all | solution.py:31
  401.8 64.6 %all_to_all.26 = bf16[8,32,16,576]{3,2,1,0:T(8,128)(2,1)} all-to-all(bf16[8,32,16,576]{3,2,1,0:T(8,128)(2,1)S(1)} %broadcast_in_dim.42), channel_id=1, replica_groups=mesh['groups'=2,'seq'=32,'head'=4,'sub'=2] {'head','sub'}, dimensions={0} | all-to-all | bytes 9437184 | tf_op jit(solution)/shard_map/all_to_all | solution.py:31
  466.4 2.6 stack.2
  469.1 10.5 all-to-all-start.2
  483.8 5.7 copy.72
  489.4 411.3 %all-to-all-done.2 = bf16[32,48,1536]{2,1,0:T(8,128)(2,1)} async-done(((bf16[32,48,1536]{2,1,0:T(8,128)(2,1)}), bf16[32,48,1536]{2,1,0:T(8,128)(2,1)}, u32[]{:S(2)}, u32[]{:S(2)}) %all-to-all-start.2) | async-done | bytes 4718624 | tf_op jit(solution)/shard_map/all_to_all | solution.py:20
  900.7 3.2 convolution_convert_fusion
  906.7 368.9 %while.21 = (s32[]{:T(128)}, f32[8,64]{1,0:T(8,128)S(1)}, f32[8,64]{1,0:T(8,128)S(1)}, f32[8,64,512]{2,1,0:T(8,128)S(1)}, f32[8,64]{1,0:T(8,128)S(1)}, /*index=5...) while((s32[]{:T(128)}, f32[8,64]{1,0:T(8,128)S(1)}, ...), condition=%wide.region_15.17_spmd, body=%wide.region_5.16_spmd.sunk | while | flops 287232768 | bytes 7917033 | solution.py:166
  916.0 2.4 conditional.4
  927.6 2.4 conditional.4
  939.3 2.4 conditional.4
  950.9 2.4 conditional.4
  962.6 2.4 conditional.4
  974.2 2.4 conditional.4
  985.8 2.4 conditional.4
  1032.4 2.4 conditional.4
  1044.1 2.4 conditional.4
  1090.7 2.4 conditional.4
  1102.3 2.4 conditional.4
  1148.9 2.4 conditional.4
  1160.5 2.4 conditional.4
  1207.1 2.4 conditional.4
  1253.7 2.4 conditional.4
  1265.4 2.4 conditional.4
  (777 shorter events, 376.2 us)
Async XLA Ops:
  6.5 122.7 %copy-start.5 = (bf16[16,1024]{1,0:T(8,128)(2,1)S(1)}, bf16[16,1024]{1,0:T(8,128)(2,1)}, u32[]{:S(2)}) copy-start(bf16[16,1024]{1,0:T(8,128)(2,1)} %param.25) | copy-start | bytes 98308
  8.4 120.8 %all-to-all-start.3 = ((bf16[32,1024,16]{1,2,0:T(8,128)(2,1)}), bf16[32,1024,16]{1,2,0:T(8,128)(2,1)S(1)}, u32[]{:S(2)}, u32[]{:S(2)}) async-start(bf16[32,1024,16]{1,2,0:T(8,128)(2,1)} %broadcast_in_dim.43), calls=%async_computation.3 | async-start | bytes 2097152 | tf_op jit(solution)/shard_map/all_to_all | solution.py:31
  14.9 267.6 %all-gather.3.cloned.1.call-start = ((), (), s32[]{:S(2)}) async-start(), calls=%async_computation.5 | async-start | bytes 4460544 | tf_op jit(solution)/shard_map/all_gather | solution.py:79
  130.4 184.7 %all-to-all-start.4 = ((bf16[32,16,1024]{2,1,0:T(8,128)(2,1)}), bf16[32,16,1024]{2,1,0:T(8,128)(2,1)S(1)}, u32[]{:S(2)}, u32[]{:S(2)}) async-start(bf16[32,16,1024]{2,1,0:T(8,128)(2,1)} %broadcast_in_dim.44), calls=%async_computation.4 | async-start | bytes 2097152 | tf_op jit(solution)/shard_map/all_to_all | solution.py:31
  287.7 9.1 copy-start.8
  296.8 18.1 %copy-start.7 = (f32[512]{0:T(512)S(1)}, f32[512]{0:T(512)}, u32[]{:S(2)}) copy-start(f32[512]{0:T(512)} %param.22) | copy-start | bytes 6148
  314.3 167.7 %copy-start.1 = (bf16[128,2112]{0,1:T(8,128)(2,1)}, bf16[128,2112]{0,1:T(8,128)(2,1)S(1)}, u32[]{:S(2)}) copy-start(bf16[128,2112]{0,1:T(8,128)(2,1)S(1)} %all_gather.7) | copy-start | bytes 1622020
  401.8 64.6 %copy-start.4 = (bf16[48,1536]{1,0:T(8,128)(2,1)S(1)}, bf16[48,1536]{1,0:T(8,128)(2,1)}, u32[]{:S(2)}) copy-start(bf16[48,1536]{1,0:T(8,128)(2,1)} %param.23) | copy-start | bytes 442372
  469.1 10.6 copy-start
  469.1 431.7 %all-to-all-start.2 = ((bf16[32,48,1536]{2,1,0:T(8,128)(2,1)}), bf16[32,48,1536]{2,1,0:T(8,128)(2,1)}, u32[]{:S(2)}, u32[]{:S(2)}) async-start(bf16[32,48,1536]{2,1,0:T(8,128)(2,1)} %stack.2), calls=%async_computation.2 | async-start | bytes 9437184 | tf_op jit(solution)/shard_map/all_to_all | solution.py:20
  483.8 417.0 %copy-start.2 = (bf16[128,2112]{0,1:T(8,128)(2,1)S(1)}, bf16[128,2112]{0,1:T(8,128)(2,1)}, u32[]{:S(2)}) copy-start(bf16[128,2112]{0,1:T(8,128)(2,1)} %copy-done.1) | copy-start | bytes 1622020
  483.8 417.0 %copy-start.6 = (f32[1536]{0:T(1024)S(1)}, f32[1536]{0:T(1024)}, u32[]{:S(2)}) copy-start(f32[1536]{0:T(1024)} %param.21) | copy-start | bytes 18436
  1275.7 1.2 copy-start.3
Sparse Core Ops, SparseCore 0:
  17.8 264.5 all-gather.2
